TPU v7x, 32 devices: a whole 2x2x4 slice. The times are simulated.
32 devices in a mesh: gx: 2 (over y), gy: 4 (over z), gz: 4 (over x, core).
Axes of the slice: x: 2, y: 2, z: 4, core: 2. Of those that a mesh axis runs over, the one named last changes fastest.
Arguments:
- node_latent: bfloat16 [2, 4, 4, 512, 128], P('gx', 'gy', 'gz'), may hold values from -6 to 6
- ghost_latent: bfloat16 [2, 4, 4, 6, 64, 128], P('gx', 'gy', 'gz'), may hold values from -6 to 6
- edge_latent: bfloat16 [2, 4, 4, 2816, 128], P('gx', 'gy', 'gz'), may hold values from -6 to 6
- senders: int32 [2, 4, 4, 2816], P('gx', 'gy', 'gz'), may hold values from 0 to 895
- receivers: int32 [2, 4, 4, 2816], P('gx', 'gy', 'gz'), may hold values from 0 to 511, never falling along the last dimension, each value on 1 to 12 neighbouring positions
- export_rows: int32 [2, 4, 4, 6, 64], P('gx', 'gy', 'gz'), may hold values from 0 to 512, as said below
- node_cotangent: bfloat16 [2, 4, 4, 512, 128], P('gx', 'gy', 'gz'), may hold values from -6 to 6
- edge_cotangent: bfloat16 [2, 4, 4, 2816, 128], P('gx', 'gy', 'gz'), may hold values from -6 to 6
- w_edge_in: bfloat16 [384, 128], replicated, may hold values from -0.3125 to 0.3125
- w_edge_hidden: bfloat16 [2, 128, 128], replicated, may hold values from -0.5 to 0.5
- b_edge: float32 [3, 128], replicated, may hold values from -3 to 3
- gain_edge: float32 [128], replicated, may hold values from 0.1 to 1.9
- shift_edge: float32 [128], replicated, may hold values from -3 to 3
- w_node_in: bfloat16 [256, 128], replicated, may hold values from -0.375 to 0.375
- w_node_hidden: bfloat16 [2, 128, 128], replicated, may hold values from -0.5 to 0.5
- b_node: float32 [3, 128], replicated, may hold values from -3 to 3
- gain_node: float32 [128], replicated, may hold values from 0.1 to 1.9
Outputs:
- node_grad: float32 [2, 4, 4, 512, 128], P('gx', 'gy', 'gz')
- edge_grad: bfloat16 [2, 4, 4, 2816, 128], P('gx', 'gy', 'gz')
- grad_w_edge_in: float32 [384, 128], replicated
- grad_w_edge_hidden: float32 [2, 128, 128], replicated
- grad_b_edge: float32 [3, 128], replicated
- grad_gain_edge: float32 [128], replicated
- grad_shift_edge: float32 [128], replicated
- grad_w_node_in: float32 [256, 128], replicated
- grad_w_node_hidden: float32 [2, 128, 128], replicated
- grad_b_node: float32 [3, 128], replicated
- grad_gain_node: float32 [128], replicated
Inputs may be any that keep to these rules, and one draw needn't show every extreme that they name: `export_rows`: for each block and face the leading slots hold distinct owned rows of that block; the remaining slots hold 512, marking an empty slot.
All inputs are finite; a program needn't handle non-finite values.
Results may differ from a plain program's by a relative error of at most 0.02.
Values sent between devices are 32-bit elements; how exact they have to be, the bound alone decides.
A program may use at most 64 MiB of HBM per device.

v0:
```python
import jax
import jax.numpy as jnp
from jax import lax
from jax.sharding import PartitionSpec as P

EPSILON = 1e-05


def from_behind(x, axis, by):
    peers = lax.axis_size(axis)
    return lax.ppermute(x, axis, [(i, (i + by) % peers) for i in range(peers)])


def matmul(left, right):
    return jnp.dot(left, right, preferred_element_type=jnp.float32)


def contract_rows(left, right):
    return lax.dot_general(
        left, right, (((0,), (0,)), ((), ())), preferred_element_type=jnp.float32
    )


def silu_parts(preact):
    sigmoid = jax.nn.sigmoid(preact)
    return (preact * sigmoid, sigmoid * (1.0 + preact * (1.0 - sigmoid)))


def norm_parts(preact):
    centred = preact - jnp.mean(preact, -1, keepdims=True)
    inv_std = lax.rsqrt(jnp.mean(centred * centred, -1, keepdims=True) + EPSILON)
    return (centred * inv_std, inv_std)


def norm_back(grad_out, gain, normed, inv_std):
    scaled = grad_out * gain
    return inv_std * (
        scaled
        - jnp.mean(scaled, -1, keepdims=True)
        - normed * jnp.mean(scaled * normed, -1, keepdims=True)
    )


def mlp_forward(inputs, w_first, w_hidden, biases):
    first_pre = matmul(inputs, w_first) + biases[0]
    first_act, first_slope = silu_parts(first_pre)
    first_out = first_act.astype(jnp.bfloat16)
    second_pre = matmul(first_out, w_hidden[0]) + biases[1]
    second_act, second_slope = silu_parts(second_pre)
    second_out = second_act.astype(jnp.bfloat16)
    final_pre = matmul(second_out, w_hidden[1]) + biases[2]
    return ((first_out, second_out, first_slope, second_slope), final_pre)


def mlp_back_inputs(final_grad, saved, w_first, w_hidden):
    first_out, second_out, first_slope, second_slope = saved
    final_round = final_grad.astype(jnp.bfloat16)
    second_grad = matmul(final_round, w_hidden[1].T) * second_slope
    second_round = second_grad.astype(jnp.bfloat16)
    first_grad = matmul(second_round, w_hidden[0].T) * first_slope
    first_round = first_grad.astype(jnp.bfloat16)
    input_grad = matmul(first_round, w_first.T)
    bias_grad = jnp.stack([jnp.sum(first_grad, 0), jnp.sum(second_grad, 0), jnp.sum(final_grad, 0)])
    return ((first_round, second_round, final_round), bias_grad, input_grad)


def mlp_back_weights(inputs, saved, rounded):
    first_weight = contract_rows(inputs, rounded[0])
    hidden_weight = jnp.stack(
        [contract_rows(saved[0], rounded[1]), contract_rows(saved[1], rounded[2])]
    )
    return (first_weight, hidden_weight)


def forward_states(node_rows, ghost_rows, edge_rows, sender_ids, receiver_ids, params):
    node_count, feature_width = node_rows.shape
    full_rows = jnp.concatenate([node_rows, ghost_rows.reshape(-1, feature_width)], 0)
    edge_inputs = jnp.concatenate([edge_rows, full_rows[sender_ids], full_rows[receiver_ids]], 1)
    edge_stored_state, edge_pre = mlp_forward(edge_inputs, params[0], params[1], params[2])
    edge_normed, edge_inv = norm_parts(edge_pre)
    edge_new = (edge_normed * params[3] + params[4]).astype(jnp.bfloat16)
    aggregate = jax.ops.segment_sum(
        edge_new.astype(jnp.float32), receiver_ids, num_segments=node_count
    ).astype(jnp.bfloat16)
    node_input_rows = jnp.concatenate([node_rows, aggregate], 1)
    node_saved, node_pre = mlp_forward(node_input_rows, params[5], params[6], params[7])
    node_normed, node_inv = norm_parts(node_pre)
    return (
        (edge_inputs, edge_stored_state, edge_normed, edge_inv),
        (node_input_rows, node_saved, node_normed, node_inv),
    )


def node_backward(node_state, node_cot, params):
    node_input_rows, node_saved, node_normed, node_inv = node_state
    upstream = node_cot.astype(jnp.float32)
    gain_grad = jnp.sum(upstream * node_normed, 0)
    final_grad = norm_back(upstream, params[8], node_normed, node_inv)
    rounded, bias_grad, input_grad = mlp_back_inputs(final_grad, node_saved, params[5], params[6])
    first_weight, hidden_weight = mlp_back_weights(node_input_rows, node_saved, rounded)
    return (input_grad, (first_weight, hidden_weight, bias_grad, gain_grad))


def edge_backward_inputs(
    edge_state, edge_cot, agg_grad, sender_ids, receiver_ids, total_rows, params
):
    edge_inputs, edge_stored_state, edge_normed, edge_inv = edge_state
    feature_width = edge_cot.shape[1]
    edge_upstream = edge_cot.astype(jnp.float32)
    new_grad = edge_upstream + agg_grad[receiver_ids]
    gain_grad = jnp.sum(new_grad * edge_normed, 0)
    shift_grad = jnp.sum(new_grad, 0)
    final_grad = norm_back(new_grad, params[3], edge_normed, edge_inv)
    rounded, bias_grad, input_grad = mlp_back_inputs(
        final_grad, edge_stored_state, params[0], params[1]
    )
    edge_grad = (edge_upstream + input_grad[:, :feature_width]).astype(jnp.bfloat16)
    full_grad = jax.ops.segment_sum(
        input_grad[:, feature_width : 2 * feature_width], sender_ids, num_segments=total_rows
    )
    full_grad = full_grad + jax.ops.segment_sum(
        input_grad[:, 2 * feature_width :], receiver_ids, num_segments=total_rows
    )
    return (edge_grad, full_grad, rounded, (bias_grad, gain_grad, shift_grad))


def send_back(ghost_grad):
    returned = []
    for side_index in range(2):
        returned.append(from_behind(ghost_grad[side_index], "gx", 1 - 2 * side_index))
    for side_index in range(2):
        returned.append(from_behind(ghost_grad[2 + side_index], "gy", 1 - 2 * side_index))
    for side_index in range(2):
        returned.append(from_behind(ghost_grad[4 + side_index], "gz", 1 - 2 * side_index))
    return returned


def on_device(
    node_latent,
    ghost_latent,
    edge_latent,
    senders,
    receivers,
    export_rows,
    node_cotangent,
    edge_cotangent,
    w_edge_in,
    w_edge_hidden,
    b_edge,
    gain_edge,
    shift_edge,
    w_node_in,
    w_node_hidden,
    b_node,
    gain_node,
):
    params = (
        w_edge_in,
        w_edge_hidden,
        b_edge,
        gain_edge,
        shift_edge,
        w_node_in,
        w_node_hidden,
        b_node,
        gain_node,
    )
    node_count = node_latent.shape[3]
    feature_width = node_latent.shape[4]
    node_rows = node_latent.reshape(node_count, feature_width)
    ghost_rows = ghost_latent.reshape(ghost_latent.shape[3:])
    edge_rows = edge_latent.reshape(edge_latent.shape[3:])
    edge_count = edge_rows.shape[0]
    sender_ids = senders.reshape(edge_count)
    receiver_ids = receivers.reshape(edge_count)
    face_rows = export_rows.reshape(export_rows.shape[3:])
    node_cot = node_cotangent.reshape(node_count, feature_width)
    edge_cot = edge_cotangent.reshape(edge_count, feature_width)
    devices = lax.axis_size("gx") * lax.axis_size("gy") * lax.axis_size("gz")
    edge_scale = float(edge_count * devices) ** (-0.5)
    node_scale = float(node_count * devices) ** (-0.5)
    total_rows = node_count + ghost_rows.shape[0] * ghost_rows.shape[1]
    edge_state, node_state = forward_states(
        node_rows, ghost_rows, edge_rows, sender_ids, receiver_ids, params
    )
    node_input_grad, node_weights = node_backward(node_state, node_cot, params)
    edge_grad, full_grad, rounded, edge_small = edge_backward_inputs(
        edge_state,
        edge_cot,
        node_input_grad[:, feature_width:],
        sender_ids,
        receiver_ids,
        total_rows,
        params,
    )
    ghost_grad = full_grad[node_count:].reshape(ghost_rows.shape)
    first_weight, hidden_weight = mlp_back_weights(edge_state[0], edge_state[1], rounded)
    returned = send_back(ghost_grad)
    edge_weights = (first_weight, hidden_weight) + edge_small
    summed = tuple(lax.psum(edge_weights + node_weights, ("gx", "gy", "gz")))
    edge_weights = summed[:5]
    node_weights = summed[5:]
    local_grad = (
        node_cot.astype(jnp.float32) + node_input_grad[:, :feature_width] + full_grad[:node_count]
    )
    for face_index in range(6):
        local_grad = local_grad.at[face_rows[face_index]].add(returned[face_index], mode="drop")
    node_grad = local_grad.reshape(node_latent.shape)
    edge_out = edge_grad.reshape(edge_latent.shape)
    return (
        node_grad,
        edge_out,
        edge_weights[0] * edge_scale,
        edge_weights[1] * edge_scale,
        edge_weights[2] * edge_scale,
        edge_weights[3] * edge_scale,
        edge_weights[4] * edge_scale,
        node_weights[0] * node_scale,
        node_weights[1] * node_scale,
        node_weights[2] * node_scale,
        node_weights[3] * node_scale,
    )


def solution(mesh):
    in_specs = (
        P("gx", "gy", "gz", None, None),
        P("gx", "gy", "gz", None, None, None),
        P("gx", "gy", "gz", None, None),
        P("gx", "gy", "gz", None),
        P("gx", "gy", "gz", None),
        P("gx", "gy", "gz", None, None),
        P("gx", "gy", "gz", None, None),
        P("gx", "gy", "gz", None, None),
        P(),
        P(),
        P(),
        P(),
        P(),
        P(),
        P(),
        P(),
        P(),
    )
    out_specs = (
        P("gx", "gy", "gz", None, None),
        P("gx", "gy", "gz", None, None),
        P(),
        P(),
        P(),
        P(),
        P(),
        P(),
        P(),
        P(),
        P(),
    )
    return jax.shard_map(
        on_device, mesh=mesh, in_specs=in_specs, out_specs=out_specs, check_vma=False
    )
```

profile of v0, /device:TPU:0, one launch (start us, length us, event | category | flops | bytes accessed | tf_op | source)
XLA Modules:
  0.0 269.4 jit_solution(13626993164029481154)
XLA Ops:
  14.5 5.6 %gather_fusion.1 = bf16[2816,128]{1,0:T(8,128)(2,1)S(1)} fusion(bf16[896,128]{1,0:T(8,128)(2,1)S(1)} %pad_maximum_fusion.4, s32[3072]{0:T(1024)S(1)} %get-tuple-element.88), kind=kCustom, calls=%fused_computation.1 | custom fusion | bytes 1453056 | tf_op jit(solution)/shard_map/gather | solution.py:78
  20.1 5.6 %gather_fusion = bf16[2816,128]{1,0:T(8,128)(2,1)S(1)} fusion(bf16[896,128]{1,0:T(8,128)(2,1)S(1)} %pad_maximum_fusion.4, s32[3072]{0:T(1024)S(1)} %pad_clamp_fusion.2), kind=kCustom, calls=%fused_computation | custom fusion | bytes 1453056 | tf_op jit(solution)/shard_map/gather | solution.py:78
  26.9 1.9 convolution_add_fusion.2
  32.0 1.6 copy.38
  33.6 19.5 %scatter_custom_fusion = f32[512,128]{1,0:T(8,128)S(1)} fusion(s32[2816]{0:T(1024)S(1)} %reduce, f32[2816,128]{1,0:T(8,128)} %copy.38, f32[]{:T(128)} %constant.8.clone.1), kind=kCustom, calls=%fused_computation.79 | custom fusion | flops 360448 | bytes 262656 | tf_op jit(solution)/shard_map/scatter-add | solution.py:82
  56.9 5.9 %gather_fusion.2 = f32[2816,128]{1,0:T(8,128)} fusion(f32[512,128]{1,0:T(8,128)S(1)} %get-tuple-element.54, s32[3072]{0:T(1024)S(1)} %get-tuple-element.87), kind=kCustom, calls=%fused_computation.2 | custom fusion | bytes 2894848 | tf_op jit(solution)/shard_map/gather | solution.py:110
  62.8 1.8 copy.41
  64.6 3.1 %multiply_reduce_fusion = (f32[128]{0:T(128)}, f32[2816]{0:T(1024)S(1)}, f32[2816]{0:T(1024)S(1)}, f32[128]{0:T(128)}) fusion(f32[2816,128]{0,1:T(8,128)S(1)} %get-tuple-element.76, f32[2816]{0:T(1024)S(1)} %add_rsqrt_fusion, f32[2816]{0:T(1024)S(1)} %broadcast_multiply_fusion.6, f32[2816,128]{0,1:T(8,128)S(1)} %copy.41, ...), kind=kLoop, calls=%fused_computation.25 | loop fusion | flops 3959040 | bytes 3651072 | tf_op jit(solution)/shard_map/reduce_sum | solution.py:111
  71.8 2.7 %fusion.12 = f32[2816,384]{1,0:T(8,128)} fusion(bf16[384,128]{1,0:T(8,128)(2,1)S(1)} %copy-done, bf16[2816,128]{1,0:T(8,128)(2,1)S(1)} %get-tuple-element.82), kind=kOutput, calls=%fused_computation.55 | convolution fusion | flops 276824064 | bytes 5144576 | tf_op jit(solution)/shard_map/dot_general | solution.py:15
  74.5 19.4 %scatter_custom_fusion.2 = f32[896,128]{1,0:T(8,128)S(1)} fusion(s32[2816]{0:T(1024)} %copy-done.23, f32[2816,384]{1,0:T(8,128)} %fusion.12, f32[]{:T(128)} %constant.8.clone.1), kind=kCustom, calls=%fused_computation.21 | custom fusion | flops 360448 | bytes 1901056 | tf_op jit(solution)/shard_map/scatter-add | solution.py:121
  94.0 15.9 %scatter_custom_fusion.1 = f32[896,128]{1,0:T(8,128)S(1)} fusion(s32[2816]{0:T(1024)} %reduce.3, f32[2816,384]{1,0:T(8,128)} %fusion.12, f32[]{:T(128)} %constant.8.clone.1), kind=kCustom, calls=%fused_computation.23 | custom fusion | flops 360448 | bytes 1901056 | tf_op jit(solution)/shard_map/scatter-add | solution.py:118
  111.1 2.4 collective-permute-start.5
  113.6 3.6 %collective-permute-start.3 = (f32[64,128]{0,1:T(8,128)}, f32[64,128]{0,1:T(8,128)}, u32[]{:S(2)}, u32[]{:S(2)}) collective-permute-start(f32[64,128]{0,1:T(8,128)} %get-tuple-element.58), channel_id=1, source_target_pairs={{0,12},{4,0},{8,4},{12,8},{1,13},{5,1},{9,5},{13,9},{2,14},{6,2},{... | collective-permute-start | bytes 98312 | tf_op jit(solution)/shard_map/ppermute | solution.py:11
  117.2 1.6 collective-permute-start
  123.4 1.5 fusion.5
  128.0 1.6 copy.54
  129.6 1.6 fusion.7
  131.5 39.2 %all-reduce = (f32[3,128]{1,0:T(4,128)S(1)}, f32[128]{0:T(128)S(1)}, f32[128]{0:T(128)S(1)}, f32[3,128]{1,0:T(4,128)S(1)}, f32[128]{0:T(128)S(1)}) all-reduce(f32[3,128]{1,0:T(4,128)S(1)} %pad_maximum_fusion.9, f32[128]{0:T(128)S(1)} %copy-done.31, f32[128]{0:T(128)S(1)} %copy-done.32, ...), channel_id=1, replica_groups=mesh['gx'=2,'gy'=4,'gz'=4] {'gx','gy','gz'}, use_global_device_ids=true, to_apply=%region_22.0 | all-reduce | flops 1152 | bytes 9216 | tf_op jit(solution)/shard_map/psum | solution.py:200
  173.0 2.3 collective-permute-start.1
  188.0 68.2 %all-reduce.4.cloned.1.call-done = (f32[384,128]{1,0:T(8,128)}, f32[2,128,128]{2,1,0:T(8,128)}, f32[256,128]{1,0:T(8,128)}, f32[2,128,128]{2,1,0:T(8,128)}) async-done(((f32[384,128]{1,0:T(8,128)}, f32[2,128,128]{2,1,0:T(8,128)}, f32[256,128]{1,0:T(8,128)}, f32[2,128,128]{2,1,0:T(8,128)}), (f32[384,128]{1,0:T(8,128)}, f32[2,128,128]{2,1,0:T(8,128)}, f32[256,128]{1,0:T(8,128)}, ...) | async-done | bytes 589840 | tf_op jit(solution)/shard_map/psum | solution.py:200
  256.2 1.6 broadcast_multiply_fusion
  257.8 1.6 broadcast_multiply_fusion.3
  259.4 1.6 broadcast_multiply_fusion.2
  261.0 1.6 broadcast_multiply_fusion.1
  (193 shorter events, 43.2 us)
Async XLA Ops:
  7.2 19.7 %copy-start = (bf16[384,128]{1,0:T(8,128)(2,1)S(1)}, bf16[384,128]{1,0:T(8,128)(2,1)}, u32[]{:S(2)}) copy-start(bf16[384,128]{1,0:T(8,128)(2,1)} %param.25) | copy-start | bytes 294916
  7.2 249.0 %all-reduce.4.cloned.1.call-start = ((), (), s32[]{:S(2)}) async-start(), calls=%async_computation | async-start | bytes 1179648 | tf_op jit(solution)/shard_map/psum | solution.py:200
  10.1 23.5 %copy-start.23 = (s32[2816]{0:T(1024)}, s32[2816]{0:T(1024)S(1)}, u32[]{:S(2)}) copy-start(s32[2816]{0:T(1024)S(1)} %reduce) | copy-start | bytes 33796
  20.1 6.8 %copy-start.9 = (bf16[2816,128]{1,0:T(8,128)(2,1)}, bf16[2816,128]{1,0:T(8,128)(2,1)S(1)}, u32[]{:S(2)}) copy-start(bf16[2816,128]{1,0:T(8,128)(2,1)S(1)} %gather_fusion.1) | copy-start | bytes 2162692
  20.1 5.6 %copy-start.8 = (bf16[1,1,1,2816,128]{4,3,2,1,0:T(8,128)(2,1)S(1)}, bf16[1,1,1,2816,128]{4,3,2,1,0:T(8,128)(2,1)}, u32[]{:S(2)}) copy-start(bf16[1,1,1,2816,128]{4,3,2,1,0:T(8,128)(2,1)} %param.24) | copy-start | bytes 2162692
  32.0 21.2 %copy-start.13 = (bf16[1,1,1,512,128]{4,3,2,1,0:T(8,128)(2,1)S(1)}, bf16[1,1,1,512,128]{4,3,2,1,0:T(8,128)(2,1)}, u32[]{:S(2)}) copy-start(bf16[1,1,1,512,128]{4,3,2,1,0:T(8,128)(2,1)} %param.17) | copy-start | bytes 393220
  32.0 21.2 %copy-start.18 = (bf16[256,128]{1,0:T(8,128)(2,1)S(1)}, bf16[256,128]{1,0:T(8,128)(2,1)}, u32[]{:S(2)}) copy-start(bf16[256,128]{1,0:T(8,128)(2,1)} %param.30) | copy-start | bytes 196612
  32.0 21.4 %copy-start.39 = (bf16[2,128,128]{2,1,0:T(8,128)(2,1)S(1)}, bf16[2,128,128]{2,1,0:T(8,128)(2,1)}, u32[]{:S(2)}) copy-start(bf16[2,128,128]{2,1,0:T(8,128)(2,1)} %param.31) | copy-start | bytes 196612
  33.5 20.1 %copy-start.40 = (bf16[2,128,128]{2,1,0:T(8,128)(2,1)S(1)}, bf16[2,128,128]{2,1,0:T(8,128)(2,1)}, u32[]{:S(2)}) copy-start(bf16[2,128,128]{2,1,0:T(8,128)(2,1)} %param.31) | copy-start | bytes 196612
  110.0 8.8 %copy-start.25 = (f32[512]{0:T(512)S(1)}, f32[512]{0:T(512)}, u32[]{:S(2)}) copy-start(f32[512]{0:T(512)} %copy-done.24) | copy-start | bytes 6148
  110.0 8.8 %copy-start.30 = (f32[128]{0:T(128)S(1)}, f32[128]{0:T(128)}, u32[]{:S(2)}) copy-start(f32[128]{0:T(128)} %param.33) | copy-start | bytes 1540
  110.2 8.5 %copy-start.44 = (f32[512,128]{1,0:T(8,128)S(1)}, f32[512,128]{1,0:T(8,128)}, u32[]{:S(2)}) copy-start(f32[512,128]{1,0:T(8,128)} %copy-done.43) | copy-start | bytes 786436
  110.3 8.8 %copy-start.17 = (f32[512,128]{1,0:T(8,128)S(1)}, f32[512,128]{1,0:T(8,128)}, u32[]{:S(2)}) copy-start(f32[512,128]{1,0:T(8,128)} %copy-done.16) | copy-start | bytes 786436
  110.3 8.8 %copy-start.46 = (bf16[512,128]{1,0:T(8,128)(2,1)S(1)}, bf16[512,128]{1,0:T(8,128)(2,1)}, u32[]{:S(2)}) copy-start(bf16[512,128]{1,0:T(8,128)(2,1)} %copy-done.45) | copy-start | bytes 393220
  111.1 74.9 %collective-permute-start.5 = (f32[64,128]{0,1:T(8,128)}, f32[64,128]{0,1:T(8,128)}, u32[]{:S(2)}, u32[]{:S(2)}) collective-permute-start(f32[64,128]{0,1:T(8,128)} %get-tuple-element.56), channel_id=1, source_target_pairs={{0,3},{1,0},{2,1},{3,2},{4,7},{5,4},{6,5},{7,6},{8,11},{9,8},{10,9... | collective-permute-start | bytes 98312 | tf_op jit(solution)/shard_map/ppermute | solution.py:11
  113.6 70.5 %collective-permute-start.4 = (f32[64,128]{0,1:T(8,128)}, f32[64,128]{0,1:T(8,128)}, u32[]{:S(2)}, u32[]{:S(2)}) collective-permute-start(f32[64,128]{0,1:T(8,128)} %get-tuple-element.57), channel_id=1, source_target_pairs={{0,1},{1,2},{2,3},{3,0},{4,5},{5,6},{6,7},{7,4},{8,9},{9,10},{10,1... | collective-permute-start | bytes 98312 | tf_op jit(solution)/shard_map/ppermute | solution.py:11
  113.6 68.5 %collective-permute-start.3 = (f32[64,128]{0,1:T(8,128)}, f32[64,128]{0,1:T(8,128)}, u32[]{:S(2)}, u32[]{:S(2)}) collective-permute-start(f32[64,128]{0,1:T(8,128)} %get-tuple-element.58), channel_id=1, source_target_pairs={{0,12},{4,0},{8,4},{12,8},{1,13},{5,1},{9,5},{13,9},{2,14},{6,2},{... | collective-permute-start | bytes 98312 | tf_op jit(solution)/shard_map/ppermute | solution.py:11
  117.1 63.0 %collective-permute-start.2 = (f32[64,128]{0,1:T(8,128)}, f32[64,128]{0,1:T(8,128)}, u32[]{:S(2)}, u32[]{:S(2)}) collective-permute-start(f32[64,128]{0,1:T(8,128)} %get-tuple-element.59), channel_id=1, source_target_pairs={{0,4},{4,8},{8,12},{12,0},{1,5},{5,9},{9,13},{13,1},{2,6},{6,10},{... | collective-permute-start | bytes 98312 | tf_op jit(solution)/shard_map/ppermute | solution.py:11
  117.1 3.2 %copy-start.7 = (bf16[2816,128]{0,1:T(8,128)(2,1)S(1)}, bf16[2816,128]{0,1:T(8,128)(2,1)}, u32[]{:S(2)}) copy-start(bf16[2816,128]{0,1:T(8,128)(2,1)} %copy-done.6) | copy-start | bytes 2162692
  117.1 3.2 %copy-start.52 = (f32[2816,128]{1,0:T(8,128)S(1)}, f32[2816,128]{1,0:T(8,128)}, u32[]{:S(2)}) copy-start(f32[2816,128]{1,0:T(8,128)} %copy-done.50) | copy-start | bytes 4325380
  117.2 55.8 %collective-permute-start = (f32[64,128]{0,1:T(8,128)}, f32[64,128]{0,1:T(8,128)}, u32[]{:S(2)}, u32[]{:S(2)}) collective-permute-start(f32[64,128]{0,1:T(8,128)} %get-tuple-element.61), channel_id=1, source_target_pairs={{0,16},{16,0},{1,17},{17,1},{2,18},{18,2},{3,19},{19,3},{4,20},{20... | collective-permute-start | bytes 98312 | tf_op jit(solution)/shard_map/ppermute | solution.py:11
  129.6 43.3 %copy-start.22 = (f32[64,128]{0,1:T(8,128)S(1)}, f32[64,128]{0,1:T(8,128)}, u32[]{:S(2)}) copy-start(f32[64,128]{0,1:T(8,128)} %get-tuple-element.60) | copy-start | bytes 98308
  173.0 6.0 %collective-permute-start.1 = (f32[64,128]{0,1:T(8,128)S(1)}, f32[64,128]{0,1:T(8,128)S(1)}, u32[]{:S(2)}, u32[]{:S(2)}) collective-permute-start(f32[64,128]{0,1:T(8,128)S(1)} %copy-done.22), channel_id=1, source_target_pairs={{0,16},{16,0},{1,17},{17,1},{2,18},{18,2},{3,19},{19,3},{4,20},{20... | collective-permute-start | bytes 98312 | tf_op jit(solution)/shard_map/ppermute | solution.py:11
  187.9 74.6 %copy-start.1 = (f32[512,128]{1,0:T(8,128)}, f32[512,128]{1,0:T(8,128)S(1)}, u32[]{:S(2)}) copy-start(f32[512,128]{1,0:T(8,128)S(1)} %scatter_fusion.5) | copy-start | bytes 786436
  (39 other events, 60.3 us)
Sparse Core Ops, SparseCore 0:
  126.3 129.8 all-reduce.3
where the time goes:
time: 271 us; the launch traced here: 269 us
  other arithmetic  82.4 us (30%)
  waiting for transfers between devices  68.3 us (25%)
  local copies, waits for them, and re-layouts  39.8 us (15%)
  blocking collectives  39.2 us (14%)
  matrix products  14.9 us (5%)
  between operations  14.8 us (5%)
  starting transfers between devices  9.93 us (4%)
    psum x1, waiting for transfers between devices, on_device(): summed = tuple(lax.psum(edge_weights + node_weights, ('gx', 'gy', 'gz')))  68.2 us
    psum x1, blocking collectives, on_device(): summed = tuple(lax.psum(edge_weights + node_weights, ('gx', 'gy', 'gz')))  39.2 us
    scatter-add x1, other arithmetic, forward_states(): jax.ops.segment_sum(edge_new.astype(jnp.float32), receiver_ids, num_segme...  19.5 us
    scatter-add x1, other arithmetic, edge_backward_inputs(): jax.ops.segment_sum(input_grad[:, 2 * feature_width:], receiver_ids, num_...  19.4 us
    scatter-add x1, other arithmetic, edge_backward_inputs(): jax.ops.segment_sum(input_grad[:, feature_width:2 * feature_width], sende...  15.9 us
    unnamed x115, local copies, waits for them, and re-layouts  11 us
    dot_general x12, matrix products, matmul(): return jnp.dot(left, right, preferred_element_type=jnp.float32)  10.7 us
    ppermute x6, starting transfers between devices, from_behind(): return lax.ppermute(x, axis, [(i, (i + by) % peers) for i in range(peers)])  9.9 us
  transfers between devices with their start and end apart: 7, of which 1 were waited for; matrix products, arithmetic and copies ran while one was open for 9% of the time, Pallas kernels for 0%

commit v1 on v0

v1 whole, which is shorter than its diff:
```python
import functools

import jax
import jax.numpy as jnp
from jax import lax
from jax.experimental import pallas as pl
from jax.experimental.pallas import tpu as pltpu
from jax.sharding import PartitionSpec as P

EPSILON = 1e-05
LANES = 128
EDGE_TILES = 2
MESH = pl.DeviceIdType.MESH
AXES = ("gx", "gy", "gz")


def matmul(left, right):
    return jnp.dot(left, right, preferred_element_type=jnp.float32)


def matmul_nt(left, right):
    return lax.dot_general(
        left, right, (((1,), (1,)), ((), ())), preferred_element_type=jnp.float32
    )


def contract_rows(left, right):
    return lax.dot_general(
        left, right, (((0,), (0,)), ((), ())), preferred_element_type=jnp.float32
    )


def silu_parts(preact):
    sigmoid = 0.5 * jnp.tanh(0.5 * preact) + 0.5
    act = preact * sigmoid
    return act, sigmoid + act * (1.0 - sigmoid)


def norm_parts(preact):
    centred = preact - jnp.mean(preact, -1, keepdims=True)
    inv_std = lax.rsqrt(jnp.mean(centred * centred, -1, keepdims=True) + EPSILON)
    return centred * inv_std, inv_std


def norm_back(grad_out, gain, normed, inv_std):
    scaled = grad_out * gain
    return inv_std * (
        scaled
        - jnp.mean(scaled, -1, keepdims=True)
        - normed * jnp.mean(scaled * normed, -1, keepdims=True)
    )


def rows_sum(values):
    return jnp.sum(values, 0, keepdims=True)


def one_hot(hit):
    return jnp.where(hit, 1.0, 0.0).astype(jnp.bfloat16)


def compute_kernel(
    edge_scale,
    node_scale,
    node,
    ghost,
    edge,
    snd,
    rcv,
    ncot,
    ecot,
    we1,
    weh,
    be,
    ge,
    se,
    wn1,
    wnh,
    bn,
    gn,
    local_o,
    ghost_o,
    edge_o,
    pack_o,
    pick,
    put,
    table,
    z1_s,
    z2_s,
    slope1_s,
    slope2_s,
    normed_s,
    inv_s,
    agg_s,
    acc,
    wacc,
    small,
):
    nodes, width = node.shape
    edges = edge.shape[0]
    ghosts = ghost.shape[0]
    total = nodes + ghosts
    bf16 = jnp.bfloat16
    tile = edges // EDGE_TILES

    lane = lax.broadcasted_iota(jnp.int32, (LANES, LANES), 1)
    sub = lax.broadcasted_iota(jnp.int32, (LANES, LANES), 0)

    def build(block, carry):
        at = pl.ds(pl.multiple_of(block * LANES, LANES), LANES)
        for ids, base, count in ((snd, 0, total), (rcv, total, nodes)):
            row = jnp.broadcast_to(ids[:, at], (LANES, LANES))
            column = jnp.transpose(row)
            for part in range(count // LANES):
                where = base + part * LANES
                pick[at, where : where + LANES] = one_hot(column == lane + part * LANES)
                put[where : where + LANES, at] = one_hot(row == sub + part * LANES)
        return carry

    lax.fori_loop(0, edges // LANES, build, 0)

    table[:nodes] = matmul(node[...], we1[width : 2 * width]).astype(bf16)
    table[nodes:total] = matmul(ghost[...], we1[width : 2 * width]).astype(bf16)
    table[total:] = matmul(node[...], we1[2 * width :]).astype(bf16)
    agg_s[...] = jnp.zeros_like(agg_s)
    acc[...] = jnp.zeros_like(acc)
    wacc[...] = jnp.zeros_like(wacc)
    small[...] = jnp.zeros_like(small)

    def forward(step, carry):
        at = pl.ds(pl.multiple_of(step * tile, LANES), tile)
        first = matmul(edge[at], we1[:width]) + matmul(pick[at], table[...]) + be[0:1]
        act, slope = silu_parts(first)
        z1 = act.astype(bf16)
        z1_s[at] = z1
        slope1_s[at] = slope
        act, slope = silu_parts(matmul(z1, weh[0]) + be[1:2])
        z2 = act.astype(bf16)
        z2_s[at] = z2
        slope2_s[at] = slope
        normed, inv = norm_parts(matmul(z2, weh[1]) + be[2:3])
        normed_s[at] = normed
        inv_s[at] = jnp.broadcast_to(inv, normed.shape)
        new = (normed * ge[...] + se[...]).astype(bf16)
        agg_s[...] += matmul(put[total:, at], new)
        return carry

    lax.fori_loop(0, EDGE_TILES, forward, 0)

    agg = agg_s[...].astype(bf16)
    first = matmul(node[...], wn1[:width]) + matmul(agg, wn1[width:]) + bn[0:1]
    act, slope1 = silu_parts(first)
    z1 = act.astype(bf16)
    act, slope2 = silu_parts(matmul(z1, wnh[0]) + bn[1:2])
    z2 = act.astype(bf16)
    normed, inv = norm_parts(matmul(z2, wnh[1]) + bn[2:3])
    up = ncot[...].astype(jnp.float32)
    gain_row = rows_sum(up * normed)
    g3 = norm_back(up, gn[...], normed, inv)
    r3 = g3.astype(bf16)
    g2 = matmul_nt(r3, wnh[1]) * slope2
    r2 = g2.astype(bf16)
    g1 = matmul_nt(r2, wnh[0]) * slope1
    r1 = g1.astype(bf16)
    local_o[...] = up + matmul_nt(r1, wn1[:width])
    agg_grad = matmul_nt(r1, wn1[width:]).astype(bf16)
    base = 5 * width
    pack_o[base : base + width] = contract_rows(node[...], r1) * node_scale
    pack_o[base + width : base + 2 * width] = contract_rows(agg, r1) * node_scale
    pack_o[base + 2 * width : base + 3 * width] = contract_rows(z1, r2) * node_scale
    pack_o[base + 3 * width : base + 4 * width] = contract_rows(z2, r3) * node_scale
    tail = 9 * width
    pack_o[tail:] = jnp.zeros((pack_o.shape[0] - tail, width), jnp.float32)
    for index, row in enumerate((rows_sum(g1), rows_sum(g2), rows_sum(g3), gain_row)):
        spot = tail + 5 + index
        pack_o[spot : spot + 1] = row * node_scale

    def backward(step, carry):
        at = pl.ds(pl.multiple_of(step * tile, LANES), tile)
        cot = ecot[at].astype(jnp.float32)
        up = cot + matmul(pick[at, total:], agg_grad)
        normed = normed_s[at]
        g3 = norm_back(up, ge[...], normed, inv_s[at])
        r3 = g3.astype(bf16)
        g2 = matmul_nt(r3, weh[1]) * slope2_s[at]
        r2 = g2.astype(bf16)
        g1 = matmul_nt(r2, weh[0]) * slope1_s[at]
        r1 = g1.astype(bf16)
        edge_o[at] = (cot + matmul_nt(r1, we1[:width])).astype(bf16)
        acc[...] += matmul(put[:, at], r1)
        wacc[:width] += contract_rows(edge[at], r1)
        wacc[width : 2 * width] += contract_rows(z1_s[at], r2)
        wacc[2 * width :] += contract_rows(z2_s[at], r3)
        for index, term in enumerate((g1, g2, g3, up * normed, up)):
            small[index : index + 1] += rows_sum(term)
        return carry

    lax.fori_loop(0, EDGE_TILES, backward, 0)

    by_sender = acc[:total].astype(bf16)
    by_receiver = acc[total:].astype(bf16)
    full = matmul_nt(by_sender, we1[width : 2 * width])
    local_o[...] += full[:nodes] + matmul_nt(by_receiver, we1[2 * width :])
    ghost_o[...] = full[nodes:]
    pack_o[:width] = wacc[:width] * edge_scale
    middle = contract_rows(node[...], by_sender[:nodes])
    middle += contract_rows(ghost[...], by_sender[nodes:])
    pack_o[width : 2 * width] = middle * edge_scale
    pack_o[2 * width : 3 * width] = contract_rows(node[...], by_receiver) * edge_scale
    pack_o[3 * width : 5 * width] = wacc[width:] * edge_scale
    pack_o[tail : tail + 5] = small[:5] * edge_scale


def stages_of(sizes):
    stages = [("gz", 2, 1), ("gz", sizes["gz"] // 2, 2), ("gx", sizes["gx"], 1)]
    stages.append(("gy", sizes["gy"], 1))
    return [stage for stage in stages if stage[1] > 1]


def member(stage):
    axis, count, stride = stage
    return lax.rem(lax.axis_index(axis) // stride, count)


def peer(stage, distance):
    axis, count, stride = stage
    mine = member(stage)
    other = lax.rem(mine + distance, count)
    return other, {axis: lax.axis_index(axis) + (other - mine) * stride}


def comm_kernel(sizes, *refs):
    stages = stages_of(sizes)
    pack, ghost, out, halo = refs[:4]
    own = refs[4]
    landing = refs[5 : 5 + len(stages)]
    sums = refs[5 + len(stages) : 5 + 2 * len(stages)]
    ssem, rsem, asem, gsem, hs, hr, lsem = refs[5 + 2 * len(stages) :]

    def face_target(face):
        axis, side = AXES[face // 2], face % 2
        count = sizes[axis]
        step = 1 if side == 0 else count - 1
        return {axis: lax.rem(lax.axis_index(axis) + step, count)}

    barrier = pltpu.get_barrier_semaphore()
    greeted = 0
    for face in range(6):
        pl.semaphore_signal(barrier, inc=1, device_id=face_target(face), device_id_type=MESH)
        greeted += 1
    for stage in stages:
        for distance in range(1, stage[1]):
            pl.semaphore_signal(
                barrier, inc=1, device_id=peer(stage, distance)[1], device_id_type=MESH
            )
            greeted += 1
    pl.semaphore_wait(barrier, greeted)

    slots = ghost.shape[0] // 6
    faces = []
    for face in range(6):
        rows = pl.ds(face * slots, slots)
        copy = pltpu.make_async_remote_copy(
            src_ref=ghost.at[rows],
            dst_ref=halo.at[rows],
            send_sem=hs.at[face],
            recv_sem=hr.at[face],
            device_id=face_target(face),
            device_id_type=MESH,
        )
        faces.append(copy)

    source = pack
    length = pack.shape[0]
    offset = 0
    segments = []
    slot = 0
    for index, stage in enumerate(stages):
        count = stage[1]
        piece = length // count
        copies = []
        for distance in range(1, count):
            other, device = peer(stage, distance)
            copy = pltpu.make_async_remote_copy(
                src_ref=source.at[pl.ds(pl.multiple_of(other * piece, 8), piece)],
                dst_ref=landing[index].at[distance - 1],
                send_sem=ssem.at[slot],
                recv_sem=rsem.at[slot],
                device_id=device,
                device_id_type=MESH,
            )
            copy.start()
            copies.append(copy)
            slot += 1
        if index == 0:
            for copy in faces:
                copy.start()
        mine = member(stage)
        for copy in copies:
            copy.wait()
        summed = source[pl.ds(pl.multiple_of(mine * piece, 8), piece)]
        for distance in range(1, count):
            summed = summed + landing[index][distance - 1]
        sums[index][...] = summed
        offset = offset + mine * piece
        segments.append((stage, offset, piece))
        source = sums[index]
        length = piece

    home = pl.ds(pl.multiple_of(offset, 8), length)
    out[home] = source[...]
    slot = 0
    for stage, start, piece in reversed(segments):
        count = stage[1]
        rows = pl.ds(pl.multiple_of(start, 8), piece)
        copies = []
        for distance in range(1, count):
            device = peer(stage, distance)[1]
            copy = pltpu.make_async_remote_copy(
                src_ref=out.at[rows],
                dst_ref=out.at[rows],
                send_sem=asem.at[slot],
                recv_sem=gsem.at[slot],
                device_id=device,
                device_id_type=MESH,
            )
            copy.start()
            copies.append(copy)
            slot += 1
        for copy in copies:
            copy.wait()
    for copy in faces:
        copy.wait()


def finish_kernel(
    packed, local, halo, faces, node_o, we1_o, weh_o, be_o, ge_o, se_o, wn1_o, wnh_o, bn_o, gn_o
):
    nodes, width = local.shape
    slots = faces.shape[1]
    spot = lax.broadcasted_iota(jnp.int32, (nodes, slots), 0)
    total = local[...]
    for face in range(6):
        hit = one_hot(spot == faces[face : face + 1])
        values = halo[face * slots : (face + 1) * slots].astype(jnp.bfloat16)
        total = total + matmul(hit, values)
    node_o[...] = total
    we1_o[...] = packed[: 3 * width]
    weh_o[0] = packed[3 * width : 4 * width]
    weh_o[1] = packed[4 * width : 5 * width]
    wn1_o[...] = packed[5 * width : 7 * width]
    wnh_o[0] = packed[7 * width : 8 * width]
    wnh_o[1] = packed[8 * width : 9 * width]
    tail = 9 * width
    be_o[...] = packed[tail : tail + 3]
    ge_o[...] = packed[tail + 3 : tail + 4]
    se_o[...] = packed[tail + 4 : tail + 5]
    bn_o[...] = packed[tail + 5 : tail + 8]
    gn_o[...] = packed[tail + 8 : tail + 9]


VMEM = pl.BlockSpec(memory_space=pltpu.VMEM)


def on_device(
    sizes,
    node_latent,
    ghost_latent,
    edge_latent,
    senders,
    receivers,
    export_rows,
    node_cotangent,
    edge_cotangent,
    w_edge_in,
    w_edge_hidden,
    b_edge,
    gain_edge,
    shift_edge,
    w_node_in,
    w_node_hidden,
    b_node,
    gain_node,
):
    f32, bf16 = jnp.float32, jnp.bfloat16
    nodes, width = node_latent.shape[3:]
    slots = ghost_latent.shape[4]
    ghosts = 6 * slots
    edges = edge_latent.shape[3]
    total = nodes + ghosts
    devices = sizes["gx"] * sizes["gy"] * sizes["gz"]
    edge_scale = float(edges * devices) ** (-0.5)
    node_scale = float(nodes * devices) ** (-0.5)
    unit = 8 * devices
    packed_rows = -(-(9 * width + 9) // unit) * unit

    def shape(*dims, dtype=f32):
        return jax.ShapeDtypeStruct(dims, dtype)

    local, ghost_grad, edge_grad, packed = pl.pallas_call(
        functools.partial(compute_kernel, edge_scale, node_scale),
        out_shape=(
            shape(nodes, width),
            shape(ghosts, width),
            shape(edges, width, dtype=bf16),
            shape(packed_rows, width),
        ),
        in_specs=[VMEM] * 16,
        out_specs=(VMEM,) * 4,
        scratch_shapes=[
            pltpu.VMEM((edges, total + nodes), bf16),
            pltpu.VMEM((total + nodes, edges), bf16),
            pltpu.VMEM((total + nodes, width), bf16),
            pltpu.VMEM((edges, width), bf16),
            pltpu.VMEM((edges, width), bf16),
            pltpu.VMEM((edges, width), f32),
            pltpu.VMEM((edges, width), f32),
            pltpu.VMEM((edges, width), f32),
            pltpu.VMEM((edges, width), f32),
            pltpu.VMEM((nodes, width), f32),
            pltpu.VMEM((total + nodes, width), f32),
            pltpu.VMEM((3 * width, width), f32),
            pltpu.VMEM((8, width), f32),
        ],
        compiler_params=pltpu.CompilerParams(vmem_limit_bytes=60 * 1024 * 1024),
        name="block_pass",
    )(
        node_latent.reshape(nodes, width),
        ghost_latent.reshape(ghosts, width),
        edge_latent.reshape(edges, width),
        senders.reshape(1, edges),
        receivers.reshape(1, edges),
        node_cotangent.reshape(nodes, width),
        edge_cotangent.reshape(edges, width),
        w_edge_in,
        w_edge_hidden,
        b_edge,
        gain_edge.reshape(1, width),
        shift_edge.reshape(1, width),
        w_node_in,
        w_node_hidden,
        b_node,
        gain_node.reshape(1, width),
    )

    stages = stages_of(sizes)
    landing, sums = [], []
    length = packed_rows
    hops = 0
    for stage in stages:
        length //= stage[1]
        landing.append(pltpu.VMEM((stage[1] - 1, length, width), f32))
        sums.append(pltpu.VMEM((length, width), f32))
        hops += stage[1] - 1
    dma = pltpu.SemaphoreType.DMA
    reduced, halo = pl.pallas_call(
        functools.partial(comm_kernel, sizes),
        out_shape=(shape(packed_rows, width), shape(ghosts, width)),
        in_specs=[VMEM] * 2,
        out_specs=(VMEM,) * 2,
        scratch_shapes=[pltpu.VMEM((8, width), f32)]
        + landing
        + sums
        + [dma((hops,)), dma((hops,)), dma((hops,)), dma((hops,)), dma((6,)), dma((6,)), dma((1,))],
        compiler_params=pltpu.CompilerParams(collective_id=0, has_side_effects=True),
        name="exchange",
    )(packed, ghost_grad)

    outs = pl.pallas_call(
        finish_kernel,
        out_shape=(
            shape(nodes, width),
            shape(3 * width, width),
            shape(2, width, width),
            shape(3, width),
            shape(1, width),
            shape(1, width),
            shape(2 * width, width),
            shape(2, width, width),
            shape(3, width),
            shape(1, width),
        ),
        in_specs=[VMEM] * 4,
        out_specs=(VMEM,) * 10,
        name="finish",
    )(reduced, local, halo, export_rows.reshape(6, slots))
    node_grad, we1, weh, be, ge, se, wn1, wnh, bn, gn = outs
    return (
        node_grad.reshape(node_latent.shape),
        edge_grad.reshape(edge_latent.shape),
        we1,
        weh,
        be,
        ge.reshape(width),
        se.reshape(width),
        wn1,
        wnh,
        bn,
        gn.reshape(width),
    )


def solution(mesh):
    block = P("gx", "gy", "gz")
    sizes = dict(mesh.shape)
    return jax.shard_map(
        functools.partial(on_device, sizes),
        mesh=mesh,
        in_specs=(block,) * 8 + (P(),) * 9,
        out_specs=(block,) * 2 + (P(),) * 9,
        check_vma=False,
    )
```

time: 271 us -> 60.5 us (0.22)
  other arithmetic: 82.4 us -> 0 us
  waiting for transfers between devices: 68.3 us -> 0 us
  Pallas kernels: 0 us -> 58.3 us
  blocking collectives: 39.2 us -> 0 us
  local copies, waits for them, and re-layouts: 39.8 us -> 1.27 us
  matrix products: 14.9 us -> 0 us
  between operations: 14.8 us -> 0.66 us
  starting transfers between devices: 9.93 us -> 0 us
    psum x1 -> x0, waiting for transfers between devices: 68.2 us -> none  [on_device(): summed = tuple(lax.psum(edge_weights + node_weights, ('gx', 'gy', 'gz')))]
    scatter-add x9 -> x0, other arithmetic: 61.1 us -> none  [the longest x1 19.5 us: forward_states(): jax.ops.segment_sum(edge_new.astype(jnp.float32), receiver_ids, num_segme...]
    pallas_call x0 -> x3, Pallas kernels: none -> 58.3 us  [the longest x1 34.9 us: on_device(): pl.pallas_call(functools.partial(comm_kernel, sizes), out_shape=(shape(pa...]
    psum x1 -> x0, blocking collectives: 39.2 us -> none  [on_device(): summed = tuple(lax.psum(edge_weights + node_weights, ('gx', 'gy', 'gz')))]
    gather x4 -> x0, local copies, waits for them, and re-layouts: 18.9 us -> none  [the longest x2 7.74 us: edge_backward_inputs(): new_grad = edge_upstream + agg_grad[receiver_ids]]
    dot_general x18 -> x0, matrix products: 14.9 us -> none  [the longest x12 10.7 us: matmul(): return jnp.dot(left, right, preferred_element_type=jnp.float32)]
    ppermute x6 -> x0, starting transfers between devices: 9.9 us -> none  [from_behind(): return lax.ppermute(x, axis, [(i, (i + by) % peers) for i in range(peers)])]
    unnamed x115 -> x3, local copies, waits for them, and re-layouts: 11 us -> 1.27 us
  transfers between devices with their start and end apart: 7 -> 0, of which waited for: 1 -> 0; matrix products, arithmetic and copies ran while one was open for 9% -> 0% of each run, Pallas kernels for 0% -> 0%
where the time goes in v1:
time: 60.5 us; the launch traced here: 60.2 us
  Pallas kernels  58.3 us (96%)
  local copies, waits for them, and re-layouts  1.27 us (2%)
  between operations  0.66 us (1%)
    pallas_call x1, Pallas kernels, on_device(): pl.pallas_call(functools.partial(comm_kernel, sizes), out_shape=(shape(pa...  34.9 us
    pallas_call x1, Pallas kernels, on_device(): pl.pallas_call(functools.partial(compute_kernel, edge_scale, node_scale),...  21 us
    pallas_call x1, Pallas kernels, on_device(): pl.pallas_call(finish_kernel, out_shape=(shape(nodes, width), shape(3 * w...  2.42 us
    unnamed x3, local copies, waits for them, and re-layouts  1.27 us

profile of v1, /device:TPU:0, one launch (start us, length us, event | category | flops | bytes accessed | tf_op | source)
XLA Modules:
  0.0 60.2 jit_solution(2588859074419397695)
XLA Ops:
  0.6 0.0 copy-start
  0.7 0.7 %copy-done = s32[1,1,1,6,64]{4,2,3,1,0:T(1,128)S(1)} copy-done((s32[1,1,1,6,64]{4,2,3,1,0:T(1,128)S(1)}, s32[1,1,1,6,64]{4,2,3,1,0:T(1,128)}, u32[]{:S(2)}) %copy-start) | copy-done | bytes 1560
  1.3 0.6 copy.30
  1.9 21.0 %block_pass.1 = (f32[512,128]{1,0:T(8,128)}, f32[384,128]{1,0:T(8,128)}, bf16[2816,128]{1,0:T(8,128)(2,1)}, f32[1280,128]{1,0:T(8,128)}) custom-call(bf16[512,128]{1,0:T(8,128)(2,1)} %bitcast.20, bf16[384,128]{1,0:T(8,128)(2,1)} %bitcast.22, bf16[2816,128]{1,0:T(8,128)(2,1)} %bitcast.18, s32[1,2816]{1,0:T(1,128)} %bitcast.24, s32[1,2816]{1,0:T(1,128)} %bitcast.25, ...), custom_call_target="tpu_custom_call" | custom-call | tf_op jit(solution)/shard_map/block_pass/pallas_call | solution.py:400
  23.0 34.9 %exchange.1 = (f32[1280,128]{1,0:T(8,128)}, f32[384,128]{1,0:T(8,128)}) custom-call(f32[1280,128]{1,0:T(8,128)} %get-tuple-element.27.refs_0_, f32[384,128]{1,0:T(8,128)} %get-tuple-element.28.refs_1_), custom_call_target="tpu_custom_call" | custom-call | tf_op jit(solution)/shard_map/exchange/pallas_call | solution.py:456
  57.8 2.4 %finish.1 = (f32[512,128]{1,0:T(8,128)}, f32[384,128]{1,0:T(8,128)}, f32[2,128,128]{2,1,0:T(8,128)}, f32[3,128]{1,0:T(4,128)}, f32[1,128]{1,0:T(1,128)}, /*index...) custom-call(f32[1280,128]{1,0:T(8,128)} %get-tuple-element.29.packed, ...), custom_call_target="tpu_custom_call" | custom-call | tf_op jit(solution)/shard_map/finish/pallas_call | solution.py:469
Async XLA Ops:
  0.6 0.7 %copy-start = (s32[1,1,1,6,64]{4,2,3,1,0:T(1,128)S(1)}, s32[1,1,1,6,64]{4,2,3,1,0:T(1,128)}, u32[]{:S(2)}) copy-start(s32[1,1,1,6,64]{4,2,3,1,0:T(1,128)} %param.22) | copy-start | bytes 4612

commit v2 on v1

v2 whole, which is shorter than its diff:
```python
import functools

import jax
import jax.numpy as jnp
from jax import lax
from jax.experimental import pallas as pl
from jax.experimental.pallas import tpu as pltpu
from jax.sharding import PartitionSpec as P

EPSILON = 1e-05
LANES = 128
FORWARD_TILES = 2
BACKWARD_TILES = 4
MESH = pl.DeviceIdType.MESH
AXES = ("gx", "gy", "gz")


def matmul(left, right):
    return jnp.dot(left, right, preferred_element_type=jnp.float32)


def matmul_nt(left, right):
    return lax.dot_general(
        left, right, (((1,), (1,)), ((), ())), preferred_element_type=jnp.float32
    )


def contract_rows(left, right):
    return lax.dot_general(
        left, right, (((0,), (0,)), ((), ())), preferred_element_type=jnp.float32
    )


def silu_parts(preact):
    sigmoid = 0.5 * jnp.tanh(0.5 * preact) + 0.5
    act = preact * sigmoid
    return act, sigmoid + act * (1.0 - sigmoid)


def norm_parts(preact):
    centred = preact - jnp.mean(preact, -1, keepdims=True)
    inv_std = lax.rsqrt(jnp.mean(centred * centred, -1, keepdims=True) + EPSILON)
    return centred * inv_std, inv_std


def norm_back(grad_out, gain, normed, inv_std):
    scaled = grad_out * gain
    return inv_std * (
        scaled
        - jnp.mean(scaled, -1, keepdims=True)
        - normed * jnp.mean(scaled * normed, -1, keepdims=True)
    )


def rows_sum(values):
    return jnp.sum(values, 0, keepdims=True)


def one_hot(hit):
    return jnp.where(hit, 1.0, 0.0).astype(jnp.bfloat16)


def stage_groups(sizes):
    core = [("gz", 2, 1)]
    near = [("gx", sizes["gx"], 1), ("gz", sizes["gz"] // 2, 2)]
    far = [("gy", sizes["gy"], 1)]
    return core, near, far


def group_size(group):
    count = 1
    for _, members, _ in group:
        count *= members
    return count


def coordinate(part):
    axis, count, stride = part
    return lax.rem(lax.axis_index(axis) // stride, count)


def member(group):
    index = 0
    for part in group:
        index = index * part[1] + coordinate(part)
    return index


def peers(group):
    steps = [()]
    for part in group:
        steps = [step + (more,) for step in steps for more in range(part[1])]
    found = []
    for step in steps[1:]:
        index = 0
        device = {}
        for part, more in zip(group, step):
            axis, count, stride = part
            mine = coordinate(part)
            other = lax.rem(mine + more, count)
            index = index * count + other
            here = device.get(axis, lax.axis_index(axis))
            device[axis] = here + (other - mine) * stride
        found.append((index, device))
    return found


class Reducer:
    def __init__(self, groups, source, out, scratch):
        self.groups = groups
        self.out = out
        self.source = source
        count = len(groups)
        self.landing = scratch[:count]
        self.sums = scratch[count : 2 * count]
        self.sems = scratch[2 * count :]
        self.length = source.shape[0]
        self.offset = 0
        self.segments = []
        self.slot = 0
        self.pending = []

    def send(self, source, target, device, sends, lands):
        copy = pltpu.make_async_remote_copy(
            src_ref=source,
            dst_ref=target,
            send_sem=self.sems[sends].at[self.slot],
            recv_sem=self.sems[lands].at[self.slot],
            device_id=device,
            device_id_type=MESH,
        )
        copy.start()
        self.pending.append(copy)
        self.slot += 1

    def wait(self):
        for copy in self.pending:
            copy.wait()
        self.pending = []

    def scatter(self):
        index = len(self.segments)
        group = self.groups[index]
        piece = self.length // group_size(group)
        for spot, (other, device) in enumerate(peers(group)):
            rows = pl.ds(pl.multiple_of(other * piece, 8), piece)
            self.send(self.source.at[rows], self.landing[index].at[spot], device, 0, 1)

    def add(self):
        index = len(self.segments)
        group = self.groups[index]
        piece = self.length // group_size(group)
        self.wait()
        mine = member(group)
        total = self.source[pl.ds(pl.multiple_of(mine * piece, 8), piece)]
        for spot in range(group_size(group) - 1):
            total = total + self.landing[index][spot]
        self.offset = self.offset + mine * piece
        self.segments.append((group, self.offset, piece))
        if len(self.segments) == len(self.groups):
            self.out[pl.ds(pl.multiple_of(self.offset, 8), piece)] = total
            self.slot = 0
        else:
            self.sums[index][...] = total
            self.source = self.sums[index]
            self.length = piece

    def gather(self):
        group, start, piece = self.segments.pop()
        rows = pl.ds(pl.multiple_of(start, 8), piece)
        for _, device in peers(group):
            self.send(self.out.at[rows], self.out.at[rows], device, 2, 3)


def reducer_scratch(groups, rows, width):
    landing, sums, hops = [], [], 0
    for group in groups:
        rows //= group_size(group)
        landing.append(pltpu.VMEM((group_size(group) - 1, rows, width), jnp.float32))
        sums.append(pltpu.VMEM((rows, width), jnp.float32))
        hops += group_size(group) - 1
    return landing + sums + [pltpu.SemaphoreType.DMA((hops,))] * 4


def split_tiles(blocks, tiles):
    sizes = [blocks // tiles + (index < blocks % tiles) for index in range(tiles)]
    starts = [sum(sizes[:index]) for index in range(tiles)]
    return [(LANES * start, LANES * size) for start, size in zip(starts, sizes)]


def face_target(sizes, face):
    axis, side = AXES[face // 2], face % 2
    count = sizes[axis]
    step = 1 if side == 0 else count - 1
    return {axis: lax.rem(lax.axis_index(axis) + step, count)}


def block_kernel(
    sizes,
    edge_scale,
    node_scale,
    node,
    ghost,
    edge,
    snd,
    rcv,
    faces,
    ncot,
    ecot,
    we1,
    weh,
    be,
    ge,
    se,
    wn1,
    wnh,
    bn,
    gn,
    node_o,
    edge_o,
    nred_o,
    ared_o,
    bred_o,
    pick,
    put,
    table,
    z1_s,
    z2_s,
    r1_s,
    slope1_s,
    slope2_s,
    normed_s,
    inv_s,
    npack,
    apack,
    bpack,
    ghost_s,
    halo,
    hsend,
    hland,
    *scratch,
):
    nodes, width = node.shape
    edges = edge.shape[0]
    ghosts = ghost.shape[0]
    slots = ghosts // 6
    total = nodes + ghosts
    bf16, f32 = jnp.bfloat16, jnp.float32
    core, near, far = stage_groups(sizes)
    third = len(scratch) // 3
    node_red = Reducer([core, near, far], npack, nred_o, scratch[:third])
    a_red = Reducer([core, near, far], apack, ared_o, scratch[third : 2 * third])
    b_red = Reducer([core, far, near], bpack, bred_o, scratch[2 * third :])

    barrier = pltpu.get_barrier_semaphore()
    greeted = [face_target(sizes, face) for face in range(6)]
    for group in (core, near, far):
        greeted += [device for _, device in peers(group)]
    for device in greeted:
        pl.semaphore_signal(barrier, inc=1, device_id=device, device_id_type=MESH)

    lane = lax.broadcasted_iota(jnp.int32, (LANES, LANES), 1)
    sub = lax.broadcasted_iota(jnp.int32, (LANES, LANES), 0)

    def build(block, carry):
        at = pl.ds(pl.multiple_of(block * LANES, LANES), LANES)
        for ids, base, count in ((snd, 0, total), (rcv, total, nodes)):
            row = jnp.broadcast_to(ids[:, at], (LANES, LANES))
            column = jnp.transpose(row)
            for part in range(count // LANES):
                where = base + part * LANES
                pick[at, where : where + LANES] = one_hot(column == lane + part * LANES)
                put[where : where + LANES, at] = one_hot(row == sub + part * LANES)
        return carry

    lax.fori_loop(0, edges // LANES, build, 0)

    table[:nodes] = matmul(node[...], we1[width : 2 * width]).astype(bf16)
    table[nodes:total] = matmul(ghost[...], we1[width : 2 * width]).astype(bf16)
    table[total:] = matmul(node[...], we1[2 * width :]).astype(bf16)

    agg = jnp.zeros((nodes, width), f32)
    for start, size in split_tiles(edges // LANES, FORWARD_TILES):
        at = pl.ds(start, size)
        first = matmul(edge[at], we1[:width]) + matmul(pick[at], table[...]) + be[0:1]
        act, slope = silu_parts(first)
        z1 = act.astype(bf16)
        z1_s[at] = z1
        slope1_s[at] = slope
        act, slope = silu_parts(matmul(z1, weh[0]) + be[1:2])
        z2 = act.astype(bf16)
        z2_s[at] = z2
        slope2_s[at] = slope
        normed, inv = norm_parts(matmul(z2, weh[1]) + be[2:3])
        normed_s[at] = normed
        inv_s[at] = jnp.broadcast_to(inv, normed.shape)
        new = (normed * ge[...] + se[...]).astype(bf16)
        agg = agg + matmul(put[total:, at], new)

    agg = agg.astype(bf16)
    first = matmul(node[...], wn1[:width]) + matmul(agg, wn1[width:]) + bn[0:1]
    act, slope1 = silu_parts(first)
    z1 = act.astype(bf16)
    act, slope2 = silu_parts(matmul(z1, wnh[0]) + bn[1:2])
    z2 = act.astype(bf16)
    normed, inv = norm_parts(matmul(z2, wnh[1]) + bn[2:3])
    up = ncot[...].astype(f32)
    gain_row = rows_sum(up * normed)
    g3 = norm_back(up, gn[...], normed, inv)
    r3 = g3.astype(bf16)
    g2 = matmul_nt(r3, wnh[1]) * slope2
    r2 = g2.astype(bf16)
    g1 = matmul_nt(r2, wnh[0]) * slope1
    r1 = g1.astype(bf16)
    node_o[...] = up + matmul_nt(r1, wn1[:width])
    agg_grad = matmul_nt(r1, wn1[width:]).astype(bf16)
    node_terms = [contract_rows(node[...], r1), contract_rows(agg, r1)]
    node_terms += [contract_rows(z1, r2), contract_rows(z2, r3)]
    for index, term in enumerate(node_terms):
        npack[index * width : (index + 1) * width] = term * node_scale
    for pack, used in ((npack, 4 * width), (apack, 4 * width), (bpack, width)):
        if pack.shape[0] > used:
            pack[used:] = jnp.zeros((pack.shape[0] - used, width), f32)
    for index, row in enumerate((rows_sum(g1), rows_sum(g2), rows_sum(g3), gain_row)):
        bpack[width + 5 + index : width + 6 + index] = row * node_scale

    pl.semaphore_wait(barrier, len(greeted))
    node_red.scatter()

    small = [jnp.zeros((1, width), f32)] * 5
    acc = jnp.zeros((total + nodes, width), f32)
    grads = [jnp.zeros((width, width), f32)] * 3
    for number, (start, size) in enumerate(split_tiles(edges // LANES, BACKWARD_TILES)):
        at = pl.ds(start, size)
        up = ecot[at].astype(f32) + matmul(pick[at, total:], agg_grad)
        normed = normed_s[at]
        g3 = norm_back(up, ge[...], normed, inv_s[at])
        r3 = g3.astype(bf16)
        g2 = matmul_nt(r3, weh[1]) * slope2_s[at]
        r2 = g2.astype(bf16)
        g1 = matmul_nt(r2, weh[0]) * slope1_s[at]
        r1 = g1.astype(bf16)
        r1_s[at] = r1
        acc = acc + matmul(put[:, at], r1)
        grads[0] = grads[0] + contract_rows(edge[at], r1)
        grads[1] = grads[1] + contract_rows(z1_s[at], r2)
        grads[2] = grads[2] + contract_rows(z2_s[at], r3)
        for index, term in enumerate((g1, g2, g3, up * normed, up)):
            small[index] = small[index] + rows_sum(term)
        if number < 3:
            node_red.add()
            if number < 2:
                node_red.scatter()
            else:
                node_red.gather()

    by_sender = acc[:total].astype(bf16)
    by_receiver = acc[total:].astype(bf16)
    middle = contract_rows(node[...], by_sender[:nodes])
    middle = middle + contract_rows(ghost[...], by_sender[nodes:])
    last = contract_rows(node[...], by_receiver)
    for index, term in enumerate((grads[0], middle, last, grads[1])):
        apack[index * width : (index + 1) * width] = term * edge_scale
    bpack[:width] = grads[2] * edge_scale
    for index, row in enumerate(small):
        bpack[width + index : width + 1 + index] = row * edge_scale
    a_red.scatter()
    b_red.scatter()

    full = matmul_nt(by_sender, we1[width : 2 * width])
    ghost_s[...] = full[nodes:]
    halos = []
    for face in range(6):
        rows = pl.ds(face * slots, slots)
        copy = pltpu.make_async_remote_copy(
            src_ref=ghost_s.at[rows],
            dst_ref=halo.at[rows],
            send_sem=hsend.at[face],
            recv_sem=hland.at[face],
            device_id=face_target(sizes, face),
            device_id_type=MESH,
        )
        halos.append(copy)
    node_red.wait()
    a_red.add()
    b_red.add()
    a_red.scatter()
    b_red.scatter()
    node_red.gather()
    for copy in halos:
        copy.start()
    node_o[...] += full[:nodes] + matmul_nt(by_receiver, we1[2 * width :])
    half = edges // 2
    at = pl.ds(0, half)
    grad = ecot[at].astype(f32) + matmul_nt(r1_s[at], we1[:width])
    edge_o[at] = grad.astype(bf16)
    a_red.add()
    a_red.scatter()
    b_red.add()
    b_red.scatter()
    node_red.wait()
    node_red.gather()
    at = pl.ds(half, edges - half)
    grad = ecot[at].astype(f32) + matmul_nt(r1_s[at], we1[:width])
    edge_o[at] = grad.astype(bf16)
    a_red.add()
    a_red.gather()
    b_red.add()
    b_red.gather()
    for copy in halos:
        copy.wait()
    spot = lax.broadcasted_iota(jnp.int32, (nodes, slots), 0)
    local = node_o[...]
    for face in range(6):
        values = halo[face * slots : (face + 1) * slots].astype(bf16)
        local = local + matmul(one_hot(spot == faces[face]), values)
    node_o[...] = local
    a_red.wait()
    a_red.gather()
    b_red.wait()
    b_red.gather()
    node_red.wait()
    a_red.wait()
    a_red.gather()
    b_red.wait()
    b_red.gather()
    a_red.wait()
    b_red.wait()


def finish_kernel(
    node, edge, nred, ared, bred, node_o, edge_o, we1_o, weh_o, be_o, ge_o, se_o, wn1_o, wnh_o, bn_o, gn_o
):
    width = node.shape[1]
    node_o[...] = node[...]
    edge_o[...] = edge[...]
    we1_o[...] = ared[: 3 * width]
    weh_o[0] = ared[3 * width : 4 * width]
    weh_o[1] = bred[:width]
    wn1_o[...] = nred[: 2 * width]
    wnh_o[0] = nred[2 * width : 3 * width]
    wnh_o[1] = nred[3 * width : 4 * width]
    be_o[...] = bred[width : width + 3]
    ge_o[...] = bred[width + 3 : width + 4]
    se_o[...] = bred[width + 4 : width + 5]
    bn_o[...] = bred[width + 5 : width + 8]
    gn_o[...] = bred[width + 8 : width + 9]


VMEM = pl.BlockSpec(memory_space=pltpu.VMEM)


def on_device(
    sizes,
    node_latent,
    ghost_latent,
    edge_latent,
    senders,
    receivers,
    export_rows,
    node_cotangent,
    edge_cotangent,
    w_edge_in,
    w_edge_hidden,
    b_edge,
    gain_edge,
    shift_edge,
    w_node_in,
    w_node_hidden,
    b_node,
    gain_node,
):
    f32, bf16 = jnp.float32, jnp.bfloat16
    nodes, width = node_latent.shape[3:]
    slots = ghost_latent.shape[4]
    ghosts = 6 * slots
    edges = edge_latent.shape[3]
    total = nodes + ghosts
    devices = sizes["gx"] * sizes["gy"] * sizes["gz"]
    edge_scale = float(edges * devices) ** (-0.5)
    node_scale = float(nodes * devices) ** (-0.5)
    unit = 8 * devices

    def padded(rows):
        return -(-rows // unit) * unit

    def shape(*dims, dtype=f32):
        return jax.ShapeDtypeStruct(dims, dtype)

    core, near, far = stage_groups(sizes)
    four, two = padded(4 * width), padded(width + 9)
    reducers = reducer_scratch([core, near, far], four, width)
    reducers += reducer_scratch([core, near, far], four, width)
    reducers += reducer_scratch([core, far, near], two, width)
    passed = pl.pallas_call(
        functools.partial(block_kernel, sizes, edge_scale, node_scale),
        out_shape=(
            shape(nodes, width),
            shape(edges, width, dtype=bf16),
            shape(four, width),
            shape(four, width),
            shape(two, width),
        ),
        in_specs=[VMEM] * 17,
        out_specs=(VMEM,) * 5,
        scratch_shapes=[
            pltpu.VMEM((edges, total + nodes), bf16),
            pltpu.VMEM((total + nodes, edges), bf16),
            pltpu.VMEM((total + nodes, width), bf16),
            pltpu.VMEM((edges, width), bf16),
            pltpu.VMEM((edges, width), bf16),
            pltpu.VMEM((edges, width), bf16),
            pltpu.VMEM((edges, width), f32),
            pltpu.VMEM((edges, width), f32),
            pltpu.VMEM((edges, width), f32),
            pltpu.VMEM((edges, width), f32),
            pltpu.VMEM((four, width), f32),
            pltpu.VMEM((four, width), f32),
            pltpu.VMEM((two, width), f32),
            pltpu.VMEM((ghosts, width), f32),
            pltpu.VMEM((ghosts, width), f32),
            pltpu.SemaphoreType.DMA((6,)),
            pltpu.SemaphoreType.DMA((6,)),
        ]
        + reducers,
        compiler_params=pltpu.CompilerParams(
            collective_id=0, has_side_effects=True, vmem_limit_bytes=60 * 1024 * 1024
        ),
        name="block_pass",
    )(
        node_latent.reshape(nodes, width),
        ghost_latent.reshape(ghosts, width),
        edge_latent.reshape(edges, width),
        senders.reshape(1, edges),
        receivers.reshape(1, edges),
        export_rows.reshape(6, 1, slots),
        node_cotangent.reshape(nodes, width),
        edge_cotangent.reshape(edges, width),
        w_edge_in,
        w_edge_hidden,
        b_edge,
        gain_edge.reshape(1, width),
        shift_edge.reshape(1, width),
        w_node_in,
        w_node_hidden,
        b_node,
        gain_node.reshape(1, width),
    )

    outs = pl.pallas_call(
        finish_kernel,
        out_shape=(
            shape(nodes, width),
            shape(edges, width, dtype=bf16),
            shape(3 * width, width),
            shape(2, width, width),
            shape(3, width),
            shape(1, width),
            shape(1, width),
            shape(2 * width, width),
            shape(2, width, width),
            shape(3, width),
            shape(1, width),
        ),
        in_specs=[VMEM] * 5,
        out_specs=(VMEM,) * 11,
        name="finish",
    )(*passed)
    node_grad, edge_grad, we1, weh, be, ge, se, wn1, wnh, bn, gn = outs
    return (
        node_grad.reshape(node_latent.shape),
        edge_grad.reshape(edge_latent.shape),
        we1,
        weh,
        be,
        ge.reshape(width),
        se.reshape(width),
        wn1,
        wnh,
        bn,
        gn.reshape(width),
    )


def solution(mesh):
    block = P("gx", "gy", "gz")
    sizes = dict(mesh.shape)
    return jax.shard_map(
        functools.partial(on_device, sizes),
        mesh=mesh,
        in_specs=(block,) * 8 + (P(),) * 9,
        out_specs=(block,) * 2 + (P(),) * 9,
        check_vma=False,
    )
```

time: 60.5 us -> 50.2 us (0.83)
  Pallas kernels: 58.3 us -> 49.4 us
  local copies, waits for them, and re-layouts: 1.27 us -> 0 us
    pallas_call x3 -> x2, Pallas kernels: 58.3 us -> 49.4 us  [the longest x1 46.9 us: on_device(): pl.pallas_call(functools.partial(block_kernel, sizes, edge_scale, node_sc...]
    unnamed x3 -> x0, local copies, waits for them, and re-layouts: 1.27 us -> none
where the time goes in v2:
time: 50.2 us; the launch traced here: 50.1 us
  Pallas kernels  49.4 us (98%)
  between operations  0.66 us (1%)
    pallas_call x1, Pallas kernels, on_device(): pl.pallas_call(functools.partial(block_kernel, sizes, edge_scale, node_sc...  46.9 us
    pallas_call x1, Pallas kernels, on_device(): pl.pallas_call(finish_kernel, out_shape=(shape(nodes, width), shape(edges...  2.56 us

profile of v2, /device:TPU:0, one launch (start us, length us, event | category | flops | bytes accessed | tf_op | source)
XLA Modules:
  0.0 50.1 jit_solution(15270475607224867493)
XLA Ops:
  0.7 46.9 %block_pass.1 = (f32[512,128]{1,0:T(8,128)}, bf16[2816,128]{1,0:T(8,128)(2,1)}, f32[512,128]{1,0:T(8,128)}, f32[512,128]{1,0:T(8,128)}, f32[256,128]{1,0:T(8,128)}) custom-call(bf16[512,128]{1,0:T(8,128)(2,1)} %bitcast.18, bf16[384,128]{1,0:T(8,128)(2,1)} %bitcast.20, bf16[2816,128]{1,0:T(8,128)(2,1)} %bitcast.16, s32[1,2816]{1,0:T(1,128)} %bitcast.21, ...), custom_call_target="tpu_custom_call" | custom-call | tf_op jit(solution)/shard_map/block_pass/pallas_call | solution.py:495
  47.5 2.6 %finish.1 = (f32[512,128]{1,0:T(8,128)}, bf16[2816,128]{1,0:T(8,128)(2,1)}, f32[384,128]{1,0:T(8,128)}, f32[2,128,128]{2,1,0:T(8,128)}, f32[3,128]{1,0:T(4,128)}...) custom-call(f32[512,128]{1,0:T(8,128)} %get-tuple-element.27.node, ...), custom_call_target="tpu_custom_call" | custom-call | tf_op jit(solution)/shard_map/finish/pallas_call | solution.py:550

commit v3 on v2

--- a/solution.py
+++ b/solution.py
@@ -61,10 +61,9 @@
 
 
 def stage_groups(sizes):
-    core = [("gz", 2, 1)]
-    near = [("gx", sizes["gx"], 1), ("gz", sizes["gz"] // 2, 2)]
+    near = [("gx", sizes["gx"], 1), ("gz", sizes["gz"], 1)]
     far = [("gy", sizes["gy"], 1)]
-    return core, near, far
+    return near, far
 
 
 def group_size(group):
@@ -234,8 +233,11 @@
     npack,
     apack,
     bpack,
+    edge_s,
+    ecot_s,
     ghost_s,
     halo,
+    loads,
     hsend,
     hland,
     *scratch,
@@ -246,31 +248,44 @@
     slots = ghosts // 6
     total = nodes + ghosts
     bf16, f32 = jnp.bfloat16, jnp.float32
-    core, near, far = stage_groups(sizes)
+    near, far = stage_groups(sizes)
     third = len(scratch) // 3
-    node_red = Reducer([core, near, far], npack, nred_o, scratch[:third])
-    a_red = Reducer([core, near, far], apack, ared_o, scratch[third : 2 * third])
-    b_red = Reducer([core, far, near], bpack, bred_o, scratch[2 * third :])
-
+    node_red = Reducer([near, far], npack, nred_o, scratch[:third])
+    a_red = Reducer([near, far], apack, ared_o, scratch[third : 2 * third])
+    b_red = Reducer([far, near], bpack, bred_o, scratch[2 * third :])
+
+    loaded = [
+        pltpu.make_async_copy(edge, edge_s, loads.at[0]),
+        pltpu.make_async_copy(ecot, ecot_s, loads.at[1]),
+    ]
+    for copy in loaded:
+        copy.start()
     barrier = pltpu.get_barrier_semaphore()
     greeted = [face_target(sizes, face) for face in range(6)]
-    for group in (core, near, far):
+    for group in (near, far):
         greeted += [device for _, device in peers(group)]
     for device in greeted:
         pl.semaphore_signal(barrier, inc=1, device_id=device, device_id_type=MESH)
 
-    lane = lax.broadcasted_iota(jnp.int32, (LANES, LANES), 1)
-    sub = lax.broadcasted_iota(jnp.int32, (LANES, LANES), 0)
+    lane = lax.broadcasted_iota(jnp.int32, (LANES, LANES), 1).astype(jnp.int16)
+    sub = lax.broadcasted_iota(jnp.int32, (LANES, LANES), 0).astype(jnp.int16)
+    one = jnp.ones((LANES, LANES), bf16)
+    zero = jnp.zeros((LANES, LANES), bf16)
 
     def build(block, carry):
         at = pl.ds(pl.multiple_of(block * LANES, LANES), LANES)
         for ids, base, count in ((snd, 0, total), (rcv, total, nodes)):
             row = jnp.broadcast_to(ids[:, at], (LANES, LANES))
-            column = jnp.transpose(row)
+            column = jnp.transpose(row).astype(jnp.int16)
+            row = row.astype(jnp.int16)
             for part in range(count // LANES):
                 where = base + part * LANES
-                pick[at, where : where + LANES] = one_hot(column == lane + part * LANES)
-                put[where : where + LANES, at] = one_hot(row == sub + part * LANES)
+                pick[at, where : where + LANES] = jnp.where(
+                    column == lane + jnp.int16(part * LANES), one, zero
+                )
+                put[where : where + LANES, at] = jnp.where(
+                    row == sub + jnp.int16(part * LANES), one, zero
+                )
         return carry
 
     lax.fori_loop(0, edges // LANES, build, 0)
@@ -279,10 +294,11 @@
     table[nodes:total] = matmul(ghost[...], we1[width : 2 * width]).astype(bf16)
     table[total:] = matmul(node[...], we1[2 * width :]).astype(bf16)
 
+    loaded[0].wait()
     agg = jnp.zeros((nodes, width), f32)
     for start, size in split_tiles(edges // LANES, FORWARD_TILES):
         at = pl.ds(start, size)
-        first = matmul(edge[at], we1[:width]) + matmul(pick[at], table[...]) + be[0:1]
+        first = matmul(edge_s[at], we1[:width]) + matmul(pick[at], table[...]) + be[0:1]
         act, slope = silu_parts(first)
         z1 = act.astype(bf16)
         z1_s[at] = z1
@@ -327,12 +343,13 @@
     pl.semaphore_wait(barrier, len(greeted))
     node_red.scatter()
 
+    loaded[1].wait()
     small = [jnp.zeros((1, width), f32)] * 5
     acc = jnp.zeros((total + nodes, width), f32)
     grads = [jnp.zeros((width, width), f32)] * 3
     for number, (start, size) in enumerate(split_tiles(edges // LANES, BACKWARD_TILES)):
         at = pl.ds(start, size)
-        up = ecot[at].astype(f32) + matmul(pick[at, total:], agg_grad)
+        up = ecot_s[at].astype(f32) + matmul(pick[at, total:], agg_grad)
         normed = normed_s[at]
         g3 = norm_back(up, ge[...], normed, inv_s[at])
         r3 = g3.astype(bf16)
@@ -342,17 +359,11 @@
         r1 = g1.astype(bf16)
         r1_s[at] = r1
         acc = acc + matmul(put[:, at], r1)
-        grads[0] = grads[0] + contract_rows(edge[at], r1)
+        grads[0] = grads[0] + contract_rows(edge_s[at], r1)
         grads[1] = grads[1] + contract_rows(z1_s[at], r2)
         grads[2] = grads[2] + contract_rows(z2_s[at], r3)
         for index, term in enumerate((g1, g2, g3, up * normed, up)):
             small[index] = small[index] + rows_sum(term)
-        if number < 3:
-            node_red.add()
-            if number < 2:
-                node_red.scatter()
-            else:
-                node_red.gather()
 
     by_sender = acc[:total].astype(bf16)
     by_receiver = acc[total:].astype(bf16)
@@ -366,6 +377,8 @@
         bpack[width + index : width + 1 + index] = row * edge_scale
     a_red.scatter()
     b_red.scatter()
+    node_red.add()
+    node_red.scatter()
 
     full = matmul_nt(by_sender, we1[width : 2 * width])
     ghost_s[...] = full[nodes:]
@@ -380,33 +393,28 @@
             device_id=face_target(sizes, face),
             device_id_type=MESH,
         )
+        copy.start()
         halos.append(copy)
-    node_red.wait()
-    a_red.add()
-    b_red.add()
-    a_red.scatter()
-    b_red.scatter()
-    node_red.gather()
-    for copy in halos:
-        copy.start()
     node_o[...] += full[:nodes] + matmul_nt(by_receiver, we1[2 * width :])
     half = edges // 2
     at = pl.ds(0, half)
-    grad = ecot[at].astype(f32) + matmul_nt(r1_s[at], we1[:width])
+    grad = ecot_s[at].astype(f32) + matmul_nt(r1_s[at], we1[:width])
     edge_o[at] = grad.astype(bf16)
     a_red.add()
     a_red.scatter()
     b_red.add()
     b_red.scatter()
-    node_red.wait()
+    node_red.add()
     node_red.gather()
     at = pl.ds(half, edges - half)
-    grad = ecot[at].astype(f32) + matmul_nt(r1_s[at], we1[:width])
+    grad = ecot_s[at].astype(f32) + matmul_nt(r1_s[at], we1[:width])
     edge_o[at] = grad.astype(bf16)
     a_red.add()
     a_red.gather()
     b_red.add()
     b_red.gather()
+    node_red.wait()
+    node_red.gather()
     for copy in halos:
         copy.wait()
     spot = lax.broadcasted_iota(jnp.int32, (nodes, slots), 0)
@@ -420,10 +428,6 @@
     b_red.wait()
     b_red.gather()
     node_red.wait()
-    a_red.wait()
-    a_red.gather()
-    b_red.wait()
-    b_red.gather()
     a_red.wait()
     b_red.wait()
 
@@ -448,6 +452,7 @@
 
 
 VMEM = pl.BlockSpec(memory_space=pltpu.VMEM)
+HBM = pl.BlockSpec(memory_space=pl.ANY)
 
 
 def on_device(
@@ -487,11 +492,11 @@
     def shape(*dims, dtype=f32):
         return jax.ShapeDtypeStruct(dims, dtype)
 
-    core, near, far = stage_groups(sizes)
+    near, far = stage_groups(sizes)
     four, two = padded(4 * width), padded(width + 9)
-    reducers = reducer_scratch([core, near, far], four, width)
-    reducers += reducer_scratch([core, near, far], four, width)
-    reducers += reducer_scratch([core, far, near], two, width)
+    reducers = reducer_scratch([near, far], four, width)
+    reducers += reducer_scratch([near, far], four, width)
+    reducers += reducer_scratch([far, near], two, width)
     passed = pl.pallas_call(
         functools.partial(block_kernel, sizes, edge_scale, node_scale),
         out_shape=(
@@ -501,7 +506,7 @@
             shape(four, width),
             shape(two, width),
         ),
-        in_specs=[VMEM] * 17,
+        in_specs=[VMEM] * 2 + [HBM] + [VMEM] * 4 + [HBM] + [VMEM] * 9,
         out_specs=(VMEM,) * 5,
         scratch_shapes=[
             pltpu.VMEM((edges, total + nodes), bf16),
@@ -517,8 +522,11 @@
             pltpu.VMEM((four, width), f32),
             pltpu.VMEM((four, width), f32),
             pltpu.VMEM((two, width), f32),
+            pltpu.VMEM((edges, width), bf16),
+            pltpu.VMEM((edges, width), bf16),
             pltpu.VMEM((ghosts, width), f32),
             pltpu.VMEM((ghosts, width), f32),
+            pltpu.SemaphoreType.DMA((2,)),
             pltpu.SemaphoreType.DMA((6,)),
             pltpu.SemaphoreType.DMA((6,)),
         ]

time: 50.2 us -> 42.8 us (0.85)
  Pallas kernels: 49.4 us -> 42 us
    pallas_call x1, Pallas kernels: 46.9 us -> 39.4 us  [on_device(): pl.pallas_call(functools.partial(block_kernel, sizes, edge_scale, node_sc...]
where the time goes in v3:
time: 42.8 us; the launch traced here: 42.6 us
  Pallas kernels  42 us (98%)
  between operations  0.66 us (2%)
    pallas_call x1, Pallas kernels, on_device(): pl.pallas_call(functools.partial(block_kernel, sizes, edge_scale, node_sc...  39.4 us
    pallas_call x1, Pallas kernels, on_device(): pl.pallas_call(finish_kernel, out_shape=(shape(nodes, width), shape(edges...  2.56 us

profile of v3, /device:TPU:0, one launch (start us, length us, event | category | flops | bytes accessed | tf_op | source)
XLA Modules:
  0.0 42.6 jit_solution(9895119260908539722)
XLA Ops:
  0.7 39.4 %block_pass.1 = (f32[512,128]{1,0:T(8,128)}, bf16[2816,128]{1,0:T(8,128)(2,1)}, f32[512,128]{1,0:T(8,128)}, f32[512,128]{1,0:T(8,128)}, f32[256,128]{1,0:T(8,128)}) custom-call(bf16[512,128]{1,0:T(8,128)(2,1)} %bitcast.18, bf16[384,128]{1,0:T(8,128)(2,1)} %bitcast.20, bf16[2816,128]{1,0:T(8,128)(2,1)} %bitcast.16, s32[1,2816]{1,0:T(1,128)} %bitcast.21, ...), custom_call_target="tpu_custom_call" | custom-call | tf_op jit(solution)/shard_map/block_pass/pallas_call | solution.py:500
  40.1 2.6 %finish.1 = (f32[512,128]{1,0:T(8,128)}, bf16[2816,128]{1,0:T(8,128)(2,1)}, f32[384,128]{1,0:T(8,128)}, f32[2,128,128]{2,1,0:T(8,128)}, f32[3,128]{1,0:T(4,128)}...) custom-call(f32[512,128]{1,0:T(8,128)} %get-tuple-element.27.node, ...), custom_call_target="tpu_custom_call" | custom-call | tf_op jit(solution)/shard_map/finish/pallas_call | solution.py:558

commit v4 on v3

--- a/solution.py
+++ b/solution.py
@@ -105,32 +105,26 @@
 
 
 class Reducer:
-    def __init__(self, groups, source, out, scratch):
-        self.groups = groups
-        self.out = out
-        self.source = source
-        count = len(groups)
-        self.landing = scratch[:count]
-        self.sums = scratch[count : 2 * count]
-        self.sems = scratch[2 * count :]
-        self.length = source.shape[0]
-        self.offset = 0
-        self.segments = []
-        self.slot = 0
+    def __init__(self, first, second, source, out, scratch):
+        self.first, self.second = first, second
+        self.source, self.out = source, out
+        self.landing, self.swap, self.part = scratch[:3]
+        self.sems = scratch[3:]
+        self.piece = source.shape[0] // group_size(first)
+        self.home = pl.ds(pl.multiple_of(member(first) * self.piece, 8), self.piece)
         self.pending = []
 
-    def send(self, source, target, device, sends, lands):
+    def send(self, source, target, device, spot, stage):
         copy = pltpu.make_async_remote_copy(
             src_ref=source,
             dst_ref=target,
-            send_sem=self.sems[sends].at[self.slot],
-            recv_sem=self.sems[lands].at[self.slot],
+            send_sem=self.sems[2 * stage].at[spot],
+            recv_sem=self.sems[2 * stage + 1].at[spot],
             device_id=device,
             device_id_type=MESH,
         )
         copy.start()
         self.pending.append(copy)
-        self.slot += 1
 
     def wait(self):
         for copy in self.pending:
@@ -138,47 +132,46 @@
         self.pending = []
 
     def scatter(self):
-        index = len(self.segments)
-        group = self.groups[index]
-        piece = self.length // group_size(group)
-        for spot, (other, device) in enumerate(peers(group)):
-            rows = pl.ds(pl.multiple_of(other * piece, 8), piece)
-            self.send(self.source.at[rows], self.landing[index].at[spot], device, 0, 1)
-
-    def add(self):
-        index = len(self.segments)
-        group = self.groups[index]
-        piece = self.length // group_size(group)
+        for spot, (other, device) in enumerate(peers(self.first)):
+            rows = pl.ds(pl.multiple_of(other * self.piece, 8), self.piece)
+            self.send(self.source.at[rows], self.landing.at[spot], device, spot, 0)
+
+    def exchange(self):
         self.wait()
-        mine = member(group)
-        total = self.source[pl.ds(pl.multiple_of(mine * piece, 8), piece)]
-        for spot in range(group_size(group) - 1):
-            total = total + self.landing[index][spot]
-        self.offset = self.offset + mine * piece
-        self.segments.append((group, self.offset, piece))
-        if len(self.segments) == len(self.groups):
-            self.out[pl.ds(pl.multiple_of(self.offset, 8), piece)] = total
-            self.slot = 0
-        else:
-            self.sums[index][...] = total
-            self.source = self.sums[index]
-            self.length = piece
+        total = self.source[self.home]
+        for spot in range(group_size(self.first) - 1):
+            total = total + self.landing[spot]
+        mine = member(self.second)
+        self.part[...] = total
+        self.swap[mine] = total
+        for spot, (_, device) in enumerate(peers(self.second)):
+            self.send(self.part, self.swap.at[mine], device, spot, 1)
 
     def gather(self):
-        group, start, piece = self.segments.pop()
-        rows = pl.ds(pl.multiple_of(start, 8), piece)
-        for _, device in peers(group):
-            self.send(self.out.at[rows], self.out.at[rows], device, 2, 3)
-
-
-def reducer_scratch(groups, rows, width):
-    landing, sums, hops = [], [], 0
-    for group in groups:
-        rows //= group_size(group)
-        landing.append(pltpu.VMEM((group_size(group) - 1, rows, width), jnp.float32))
-        sums.append(pltpu.VMEM((rows, width), jnp.float32))
-        hops += group_size(group) - 1
-    return landing + sums + [pltpu.SemaphoreType.DMA((hops,))] * 4
+        self.wait()
+        total = self.swap[0]
+        for index in range(1, group_size(self.second)):
+            total = total + self.swap[index]
+        self.out[self.home] = total
+        for spot, (_, device) in enumerate(peers(self.first)):
+            self.send(self.out.at[self.home], self.out.at[self.home], device, spot, 2)
+
+
+def reducer_scratch(first, second, rows, width):
+    one, two = group_size(first), group_size(second)
+    piece = rows // one
+    dma = pltpu.SemaphoreType.DMA
+    return [
+        pltpu.VMEM((one - 1, piece, width), jnp.float32),
+        pltpu.VMEM((two, piece, width), jnp.float32),
+        pltpu.VMEM((piece, width), jnp.float32),
+        dma((one - 1,)),
+        dma((one - 1,)),
+        dma((two - 1,)),
+        dma((two - 1,)),
+        dma((one - 1,)),
+        dma((one - 1,)),
+    ]
 
 
 def split_tiles(blocks, tiles):
@@ -250,9 +243,9 @@
     bf16, f32 = jnp.bfloat16, jnp.float32
     near, far = stage_groups(sizes)
     third = len(scratch) // 3
-    node_red = Reducer([near, far], npack, nred_o, scratch[:third])
-    a_red = Reducer([near, far], apack, ared_o, scratch[third : 2 * third])
-    b_red = Reducer([far, near], bpack, bred_o, scratch[2 * third :])
+    node_red = Reducer(near, far, npack, nred_o, scratch[:third])
+    a_red = Reducer(near, far, apack, ared_o, scratch[third : 2 * third])
+    b_red = Reducer(far, near, bpack, bred_o, scratch[2 * third :])
 
     loaded = [
         pltpu.make_async_copy(edge, edge_s, loads.at[0]),
@@ -377,8 +370,7 @@
         bpack[width + index : width + 1 + index] = row * edge_scale
     a_red.scatter()
     b_red.scatter()
-    node_red.add()
-    node_red.scatter()
+    node_red.exchange()
 
     full = matmul_nt(by_sender, we1[width : 2 * width])
     ghost_s[...] = full[nodes:]
@@ -400,21 +392,12 @@
     at = pl.ds(0, half)
     grad = ecot_s[at].astype(f32) + matmul_nt(r1_s[at], we1[:width])
     edge_o[at] = grad.astype(bf16)
-    a_red.add()
-    a_red.scatter()
-    b_red.add()
-    b_red.scatter()
-    node_red.add()
+    a_red.exchange()
+    b_red.exchange()
     node_red.gather()
     at = pl.ds(half, edges - half)
     grad = ecot_s[at].astype(f32) + matmul_nt(r1_s[at], we1[:width])
     edge_o[at] = grad.astype(bf16)
-    a_red.add()
-    a_red.gather()
-    b_red.add()
-    b_red.gather()
-    node_red.wait()
-    node_red.gather()
     for copy in halos:
         copy.wait()
     spot = lax.broadcasted_iota(jnp.int32, (nodes, slots), 0)
@@ -423,9 +406,7 @@
         values = halo[face * slots : (face + 1) * slots].astype(bf16)
         local = local + matmul(one_hot(spot == faces[face]), values)
     node_o[...] = local
-    a_red.wait()
     a_red.gather()
-    b_red.wait()
     b_red.gather()
     node_red.wait()
     a_red.wait()
@@ -484,19 +465,19 @@
     devices = sizes["gx"] * sizes["gy"] * sizes["gz"]
     edge_scale = float(edges * devices) ** (-0.5)
     node_scale = float(nodes * devices) ** (-0.5)
-    unit = 8 * devices
-
-    def padded(rows):
+
+    def padded(rows, group):
+        unit = 8 * group_size(group)
         return -(-rows // unit) * unit
 
     def shape(*dims, dtype=f32):
         return jax.ShapeDtypeStruct(dims, dtype)
 
     near, far = stage_groups(sizes)
-    four, two = padded(4 * width), padded(width + 9)
-    reducers = reducer_scratch([near, far], four, width)
-    reducers += reducer_scratch([near, far], four, width)
-    reducers += reducer_scratch([far, near], two, width)
+    four, two = padded(4 * width, near), padded(width + 9, far)
+    reducers = reducer_scratch(near, far, four, width)
+    reducers += reducer_scratch(near, far, four, width)
+    reducers += reducer_scratch(far, near, two, width)
     passed = pl.pallas_call(
         functools.partial(block_kernel, sizes, edge_scale, node_scale),
         out_shape=(

time: 42.8 us -> 40.6 us (0.949)
  Pallas kernels: 42 us -> 39.8 us
    pallas_call x1, Pallas kernels: 39.4 us -> 37.3 us  [on_device(): pl.pallas_call(functools.partial(block_kernel, sizes, edge_scale, node_sc...]
where the time goes in v4:
time: 40.6 us; the launch traced here: 40.5 us
  Pallas kernels  39.8 us (98%)
  between operations  0.66 us (2%)
    pallas_call x1, Pallas kernels, on_device(): pl.pallas_call(functools.partial(block_kernel, sizes, edge_scale, node_sc...  37.3 us
    pallas_call x1, Pallas kernels, on_device(): pl.pallas_call(finish_kernel, out_shape=(shape(nodes, width), shape(edges...  2.54 us

profile of v4, /device:TPU:0, one launch (start us, length us, event | category | flops | bytes accessed | tf_op | source)
XLA Modules:
  0.0 40.5 jit_solution(17029419554173345392)
XLA Ops:
  0.7 37.3 %block_pass.1 = (f32[512,128]{1,0:T(8,128)}, bf16[2816,128]{1,0:T(8,128)(2,1)}, f32[512,128]{1,0:T(8,128)}, f32[512,128]{1,0:T(8,128)}, f32[160,128]{1,0:T(8,128)}) custom-call(bf16[512,128]{1,0:T(8,128)(2,1)} %bitcast.18, bf16[384,128]{1,0:T(8,128)(2,1)} %bitcast.20, bf16[2816,128]{1,0:T(8,128)(2,1)} %bitcast.16, s32[1,2816]{1,0:T(1,128)} %bitcast.21, ...), custom_call_target="tpu_custom_call" | custom-call | tf_op jit(solution)/shard_map/block_pass/pallas_call | solution.py:481
  37.9 2.5 %finish.1 = (f32[512,128]{1,0:T(8,128)}, bf16[2816,128]{1,0:T(8,128)(2,1)}, f32[384,128]{1,0:T(8,128)}, f32[2,128,128]{2,1,0:T(8,128)}, f32[3,128]{1,0:T(4,128)}...) custom-call(f32[512,128]{1,0:T(8,128)} %get-tuple-element.27.node, ...), custom_call_target="tpu_custom_call" | custom-call | tf_op jit(solution)/shard_map/finish/pallas_call | solution.py:539
